TPU v7x, 32 devices: a whole 2x2x4 slice. The times are simulated.
32 devices in a mesh: gx: 4 (over z), gy: 4 (over y, x), gz: 2 (over core).
Axes of the slice: x: 2, y: 2, z: 4, core: 2. Of those that a mesh axis runs over, the one named last changes fastest.
Arguments:
- pair: bfloat16 [128, 128, 128], P('gx', ('gy', 'gz')), may hold values from -6 to 6
- pair_mask: int32 [128, 128], P('gx', ('gy', 'gz')), may hold values 0 or 1
- in_gain: float32 [128], replicated, may hold values from 0.1 to 1.9
- in_bias: float32 [128], replicated, may hold values from -3 to 3
- proj_weight: bfloat16 [128, 512], replicated, may hold values from -0.5 to 0.5
- gate_weight: bfloat16 [128, 128], replicated, may hold values from -0.5 to 0.5
- out_gain: float32 [128], replicated, may hold values from 0.1 to 1.9
- out_bias: float32 [128], replicated, may hold values from -3 to 3
- out_weight: bfloat16 [128, 128], replicated, may hold values from -0.5 to 0.5
Outputs:
- update: bfloat16 [128, 128, 128], P('gx', ('gy', 'gz'))
All inputs are finite; a program needn't handle non-finite values. No bound on the sum of `pair_mask` on one device may be relied on, other than what follows from the above.
Results may differ from a plain program's by a relative error of at most 0.0071.
Values may be sent and summed in bfloat16 or wider, within the bound.
A program may use at most 64 MiB of HBM per device.

v0:
```python
import jax
import jax.numpy as jnp
from jax import lax
from jax.sharding import PartitionSpec as P


def normalize(values, gain, bias):
    average = jnp.mean(values, axis=-1, keepdims=True)
    centered = values - average
    variance = jnp.mean(centered * centered, axis=-1, keepdims=True)
    return centered * lax.rsqrt(variance + 1e-05) * gain + bias


def project(tile, mask_value, in_gain, in_bias, proj_weight):
    hidden = proj_weight.shape[1] // 4
    normed = normalize(tile.astype(jnp.float32), in_gain, in_bias).astype(jnp.bfloat16)
    projected = jnp.einsum("rwc,cd->rwd", normed, proj_weight, preferred_element_type=jnp.float32)
    left_side = (
        jax.nn.sigmoid(projected[:, :, :hidden]) * projected[:, :, hidden : 2 * hidden] * mask_value
    ).astype(jnp.bfloat16)
    right_side = (
        jax.nn.sigmoid(projected[:, :, 2 * hidden : 3 * hidden])
        * projected[:, :, 3 * hidden :]
        * mask_value
    ).astype(jnp.bfloat16)
    return (normed, left_side, right_side)


def on_device(
    pair, pair_mask, in_gain, in_bias, proj_weight, gate_weight, out_gain, out_bias, out_weight
):
    mask_value = pair_mask.astype(jnp.float32)[:, :, None]
    normed, left_side, own_right = project(pair, mask_value, in_gain, in_bias, proj_weight)
    left_slab, right_slab = (
        lax.all_gather(left_side, "gy", axis=1, tiled=True),
        lax.all_gather(own_right, "gy", axis=1, tiled=True),
    )
    every_row = lax.all_gather(own_right, "gx", axis=0, tiled=True)
    row_panel = lax.all_to_all(every_row, "gy", split_axis=0, concat_axis=1, tiled=True)
    summed = lax.psum_scatter(
        jnp.einsum("jkc,ikc->jic", row_panel, left_slab, preferred_element_type=jnp.float32),
        "gz",
        scatter_dimension=0,
        tiled=True,
    )
    triangle = jnp.transpose(summed, (1, 0, 2))
    tri_normed = normalize(triangle, out_gain, out_bias).astype(jnp.bfloat16)
    gating = jax.nn.sigmoid(
        jnp.einsum("rwc,cd->rwd", normed, gate_weight, preferred_element_type=jnp.float32)
    )
    mixed = jnp.einsum("rwh,hc->rwc", tri_normed, out_weight, preferred_element_type=jnp.float32)
    return (gating * mixed).astype(jnp.bfloat16)


def solution(mesh):
    return jax.shard_map(
        on_device,
        mesh=mesh,
        in_specs=(
            P("gx", ("gy", "gz"), None),
            P("gx", ("gy", "gz")),
            P(),
            P(),
            P(),
            P(),
            P(),
            P(),
            P(),
        ),
        out_specs=P("gx", ("gy", "gz"), None),
        check_vma=False,
    )
```

profile of v0, /device:TPU:0, one launch (start us, length us, event | category | flops | bytes accessed | tf_op | source)
XLA Modules:
  0.0 80.6 jit_solution(6983659560410940790)
XLA Ops:
  6.5 0.0 copy-start
  6.5 1.1 %convert_reduce_fusion = f32[32,16]{1,0:T(8,128)S(1)} fusion(bf16[32,16,128]{2,1,0:T(8,128)(2,1)} %param.9), kind=kLoop, calls=%fused_computation.8 | loop fusion | flops 130560 | bytes 133120 | tf_op jit(solution)/shard_map/reduce_sum | solution.py:8
  7.6 0.1 copy.52
  7.7 0.1 copy.53
  7.8 1.1 %fusion.6 = f32[32,16]{1,0:T(8,128)S(1)} fusion(bf16[32,16,128]{2,1,0:T(8,128)(2,1)} %param.9, f32[32,16]{1,0:T(8,128)S(1)} %copy.53), kind=kLoop, calls=%fused_computation.11 | loop fusion | flops 261632 | bytes 135168 | tf_op jit(solution)/shard_map/reduce_sum | solution.py:10
  8.9 0.1 copy.54
  9.0 0.1 copy.55
  9.1 0.7 convert_element_type.23
  9.8 0.1 copy.56
  9.9 0.0 copy-done
  9.9 1.3 %fusion.20 = f32[32,16,512]{2,1,0:T(8,128)S(1)} fusion(bf16[128,512]{1,0:T(8,128)(2,1)S(1)} %copy-done, bf16[32,16,128]{2,1,0:T(8,128)(2,1)} %param.9, f32[128]{0:T(128)} %param.12, f32[128]{0:T(128)} %param.11, f32[32,16]{1,0:T(8,128)S(1)} %copy.55, f32[32,16]{1,0:T(8,128)S(1)} %copy.53), kind=kOutput, calls=%fused_computation.33 | convolution fusion | flops 67502080 | bytes 1315840 | tf_op jit(solution)/shard_map/rwc,cd->rwd/dot_general | solution.py:17
  11.2 0.2 fusion.11
  11.3 18.0 %all_gather.7 = bf16[128,16,128]{2,1,0:T(8,128)(2,1)} all-gather(bf16[32,16,128]{2,1,0:T(8,128)(2,1)S(1)} %get-tuple-element.5), channel_id=1, replica_groups=mesh['gx'=4,'gy'=4,'gz'=2] {'gx'}, dimensions={0}, use_global_device_ids=true | all-gather | bytes 655360 | tf_op jit(solution)/shard_map/all_gather | solution.py:38
  29.3 3.7 %all-to-all-start = ((bf16[128,16,128]{2,1,0:T(8,128)(2,1)}), bf16[128,16,128]{2,1,0:T(8,128)(2,1)S(1)}, u32[]{:S(2)}, u32[]{:S(2)}) async-start(bf16[128,16,128]{2,1,0:T(8,128)(2,1)} %all_gather.7), calls=%async_computation | async-start | bytes 1048576 | tf_op jit(solution)/shard_map/all_to_all | solution.py:39
  33.1 0.0 reduce-scatter.2.cloned.1.call-start
  33.1 15.6 %all_gather.6 = bf16[32,64,128]{2,1,0:T(8,128)(2,1)S(1)} all-gather(bf16[32,16,128]{2,1,0:T(8,128)(2,1)S(1)} %get-tuple-element.6), channel_id=1, replica_groups=mesh['gx'=4,'gy'=4,'gz'=2] {'gy'}, dimensions={1}, use_global_device_ids=true | all-gather | bytes 655360 | tf_op jit(solution)/shard_map/all_gather | solution.py:35
  48.7 3.2 %copy.58 = bf16[32,64,128]{0,1,2:T(8,128)(2,1)S(1)} copy(bf16[32,64,128]{2,1,0:T(8,128)(2,1)S(1)} %all_gather.6) | data formatting | bytes 1048576 | tf_op jit(solution)/shard_map/all_gather | solution.py:35
  51.9 0.0 all-to-all-done
  51.9 0.9 %copy.57 = bf16[32,4,16,128]{3,2,1,0:T(8,128)(2,1)} copy(bf16[32,4,16,128]{3,2,0,1:T(8,128)(2,1)S(1)} %bitcast.25) | data formatting | bytes 1048576 | tf_op jit(solution)/shard_map/all_to_all | solution.py:39
  52.8 2.5 %copy.59 = bf16[32,64,128]{1,0,2:T(8,128)(2,1)S(1)} copy(bf16[32,64,128]{2,1,0:T(8,128)(2,1)} %bitcast.24) | data formatting | bytes 1048576 | tf_op jit(solution)/shard_map/all_to_all | solution.py:39
  55.2 2.1 %convolution_bitcast_fusion = f32[32,32,128]{0,1,2:T(8,128)} fusion(bf16[32,64,128]{0,1,2:T(8,128)(2,1)S(1)} %copy.58, bf16[32,64,128]{1,0,2:T(8,128)(2,1)S(1)} %copy.59), kind=kOutput, calls=%fused_computation | convolution fusion | flops 16777216 | bytes 1572864 | tf_op jit(solution)/shard_map/jkc,ikc->jic/dot_general | solution.py:41
  57.3 0.0 copy-start.1
  57.3 0.0 copy-start.3
  57.3 0.0 copy-start.4
  57.3 0.0 copy-start.7
  57.3 0.0 copy-start.5
  57.4 0.0 copy-start.6
  57.4 3.7 %copy.60 = f32[32,32,128]{2,1,0:T(8,128)} copy(f32[32,32,128]{0,1,2:T(8,128)} %convolution_bitcast_fusion) | data formatting | bytes 1048576 | tf_op jit(solution)/shard_map/jkc,ikc->jic/transpose | solution.py:41
  61.1 0.0 copy-start.2
  61.1 0.0 reduce-scatter.2.cloned.1.call-update
  61.1 0.0 copy-done.1
  61.1 0.0 copy-done.3
  61.1 0.0 copy-done.4
  61.1 0.0 copy-done.7
  61.1 0.3 fusion.2
  61.5 7.9 %reduce-scatter.2.cloned.1.call-done = f32[16,32,128]{2,1,0:T(8,128)} async-done(((f32[32,32,128]{2,1,0:T(8,128)}), f32[16,32,128]{2,1,0:T(8,128)}) %reduce-scatter.2.cloned.1.call-update) | async-done | bytes 262160 | tf_op jit(solution)/shard_map/reduce_scatter | solution.py:40
  69.4 1.1 %bitcast_reduce_fusion = f32[32,16]{0,1:T(8,128)S(1)} fusion(f32[16,32,128]{2,1,0:T(8,128)} %reduce-scatter.2.cloned.1.call-done), kind=kLoop, calls=%fused_computation.30 | loop fusion | flops 65024 | bytes 264192 | tf_op jit(solution)/shard_map/reduce_sum | solution.py:8
  70.5 1.2 %multiply_reduce_fusion = f32[32,16]{0,1:T(8,128)S(1)} fusion(f32[16,32,128]{2,1,0:T(8,128)} %reduce-scatter.2.cloned.1.call-done, f32[32,16]{0,1:T(8,128)S(1)} %broadcast_multiply_fusion), kind=kLoop, calls=%fused_computation.32 | loop fusion | flops 196096 | bytes 266240 | tf_op jit(solution)/shard_map/reduce_sum | solution.py:10
  71.7 0.0 copy-done.5
  71.7 0.0 copy-done.6
  71.7 1.2 %add_convert_fusion = bf16[32,16,128]{2,0,1:T(8,128)(2,1)S(1)} fusion(f32[16,32,128]{2,1,0:T(8,128)} %reduce-scatter.2.cloned.1.call-done, f32[128]{0:T(128)S(1)} %copy-done.5, f32[128]{0:T(128)S(1)} %copy-done.6, f32[32,16]{0,1:T(8,128)S(1)} %add_rsqrt_fusion, f32[32,16]{0,1:T(8,128)S(1)} %broadcast_multiply_fusion), kind=kLoop, calls=%fused_computation.31 | loop fusion | flops 327680 | bytes 398336 | tf_op jit(solution)/shard_map/convert_element_type | solution.py:47
  72.9 0.0 copy-done.2
  72.9 0.8 %fusion.3 = bf16[32,16,128]{2,1,0:T(8,128)(2,1)} fusion(f32[32,16,128]{2,1,0:T(8,128)S(1)} %fusion.2, bf16[32,16,128]{2,0,1:T(8,128)(2,1)S(1)} %add_convert_fusion, bf16[128,128]{1,0:T(8,128)(2,1)S(1)} %copy-done.2), kind=kOutput, calls=%fused_computation.6 | convolution fusion | flops 16908288 | bytes 557056 | tf_op jit(solution)/shard_map/rwh,hc->rwc/dot_general | solution.py:51
  (4 shorter events, 0.0 us)
Async XLA Ops:
  6.5 3.3 %copy-start = (bf16[128,512]{1,0:T(8,128)(2,1)S(1)}, bf16[128,512]{1,0:T(8,128)(2,1)}, u32[]{:S(2)}) copy-start(bf16[128,512]{1,0:T(8,128)(2,1)} %param.13) | copy-start | bytes 393220
  29.3 22.6 %all-to-all-start = ((bf16[128,16,128]{2,1,0:T(8,128)(2,1)}), bf16[128,16,128]{2,1,0:T(8,128)(2,1)S(1)}, u32[]{:S(2)}, u32[]{:S(2)}) async-start(bf16[128,16,128]{2,1,0:T(8,128)(2,1)} %all_gather.7), calls=%async_computation | async-start | bytes 1048576 | tf_op jit(solution)/shard_map/all_to_all | solution.py:39
  33.1 36.3 %reduce-scatter.2.cloned.1.call-start = ((), (), s32[]{:S(2)}) async-start(), calls=%async_computation.2 | async-start | bytes 786432 | tf_op jit(solution)/shard_map/reduce_scatter | solution.py:40
  57.3 3.8 %copy-start.1 = (bf16[32,16,128]{2,1,0:T(8,128)(2,1)S(1)}, bf16[32,16,128]{2,1,0:T(8,128)(2,1)}, u32[]{:S(2)}) copy-start(bf16[32,16,128]{2,1,0:T(8,128)(2,1)} %param.9) | copy-start | bytes 393220
  57.3 3.8 %copy-start.3 = (f32[128]{0:T(128)S(1)}, f32[128]{0:T(128)}, u32[]{:S(2)}) copy-start(f32[128]{0:T(128)} %param.12) | copy-start | bytes 1540
  57.3 3.8 %copy-start.4 = (f32[128]{0:T(128)S(1)}, f32[128]{0:T(128)}, u32[]{:S(2)}) copy-start(f32[128]{0:T(128)} %param.11) | copy-start | bytes 1540
  57.3 3.8 %copy-start.7 = (bf16[128,128]{1,0:T(8,128)(2,1)S(1)}, bf16[128,128]{1,0:T(8,128)(2,1)}, u32[]{:S(2)}) copy-start(bf16[128,128]{1,0:T(8,128)(2,1)} %param.14) | copy-start | bytes 98308
  57.3 14.4 %copy-start.5 = (f32[128]{0:T(128)S(1)}, f32[128]{0:T(128)}, u32[]{:S(2)}) copy-start(f32[128]{0:T(128)} %param.16) | copy-start | bytes 1540
  57.4 14.4 %copy-start.6 = (f32[128]{0:T(128)S(1)}, f32[128]{0:T(128)}, u32[]{:S(2)}) copy-start(f32[128]{0:T(128)} %param.15) | copy-start | bytes 1540
  61.1 11.8 %copy-start.2 = (bf16[128,128]{1,0:T(8,128)(2,1)S(1)}, bf16[128,128]{1,0:T(8,128)(2,1)}, u32[]{:S(2)}) copy-start(bf16[128,128]{1,0:T(8,128)(2,1)} %param.17) | copy-start | bytes 98308
Sparse Core Ops, SparseCore 0:
  61.2 8.1 reduce-scatter.1
where the time goes:
time: 81.1 us; the launch traced here: 80.6 us
  blocking collectives  33.6 us (41%)
  between operations  13.6 us (17%)
  local copies, waits for them, and re-layouts  10.6 us (13%)
  waiting for transfers between devices  7.94 us (10%)
  other arithmetic  6.58 us (8%)
  matrix products  4.53 us (6%)
  starting transfers between devices  3.72 us (5%)
    all_gather x1, blocking collectives, on_device(): every_row = lax.all_gather(own_right, 'gx', axis=0, tiled=True)  18 us
    all_gather x1, blocking collectives, on_device(): lax.all_gather(left_side, 'gy', axis=1, tiled=True)  15.6 us
    reduce_scatter x1, waiting for transfers between devices, on_device(): lax.psum_scatter(jnp.einsum('jkc,ikc->jic', row_panel, left_slab, preferr...  7.92 us
    all_to_all x1, starting transfers between devices, on_device(): lax.all_to_all(every_row, 'gy', split_axis=0, concat_axis=1, tiled=True)  3.72 us
    transpose x1, local copies, waits for them, and re-layouts, on_device(): jnp.einsum('jkc,ikc->jic', row_panel, left_slab, preferred_element_type=j...  3.7 us
    all_to_all x2, local copies, waits for them, and re-layouts, on_device(): lax.all_to_all(every_row, 'gy', split_axis=0, concat_axis=1, tiled=True)  3.31 us
    all_gather x1, local copies, waits for them, and re-layouts, on_device(): lax.all_gather(left_side, 'gy', axis=1, tiled=True)  3.21 us
    reduce_sum x2, other arithmetic, normalize(): variance = jnp.mean(centered * centered, axis=-1, keepdims=True)  2.36 us
  transfers between devices with their start and end apart: 2, of which 1 were waited for; matrix products, arithmetic and copies ran while one was open for 4% of the time, Pallas kernels for 0%

commit v1 on v0

--- a/solution.py
+++ b/solution.py
@@ -32,7 +32,7 @@
     mask_value = pair_mask.astype(jnp.float32)[:, :, None]
     normed, left_side, own_right = project(pair, mask_value, in_gain, in_bias, proj_weight)
     left_slab, right_slab = (
-        lax.all_gather(left_side, "gy", axis=1, tiled=True),
+        jnp.concatenate(lax.all_gather(left_side, "gy"), axis=1),
         lax.all_gather(own_right, "gy", axis=1, tiled=True),
     )
     every_row = lax.all_gather(own_right, "gx", axis=0, tiled=True)

time: 81.1 us -> 74.8 us (0.922)
  local copies, waits for them, and re-layouts: 10.6 us -> 6.89 us
  blocking collectives: 33.6 us -> 31.7 us
    all_gather x1 -> x0, local copies, waits for them, and re-layouts: 3.21 us -> none  [on_device(): lax.all_gather(left_side, 'gy', axis=1, tiled=True)]
    all_gather x1, blocking collectives: 15.6 us -> 13.6 us  [on_device(): lax.all_gather(left_side, 'gy')]
    reshape x0 -> x2, local copies, waits for them, and re-layouts: none -> 1.68 us  [on_device(): jnp.concatenate(lax.all_gather(left_side, 'gy'), axis=1)]
    transpose x1, local copies, waits for them, and re-layouts: 3.7 us -> 2.21 us  [on_device(): jnp.einsum('jkc,ikc->jic', row_panel, left_slab, preferred_element_type=j...]
  transfers between devices with their start and end apart: 2 -> 2, of which waited for: 1 -> 1; matrix products, arithmetic and copies ran while one was open for 4% -> 3% of each run, Pallas kernels for 0% -> 0%
where the time goes in v1:
time: 74.8 us; the launch traced here: 74.4 us
  blocking collectives  31.7 us (42%)
  between operations  13.6 us (18%)
  waiting for transfers between devices  7.63 us (10%)
  local copies, waits for them, and re-layouts  6.89 us (9%)
  other arithmetic  6.58 us (9%)
  matrix products  4.34 us (6%)
  starting transfers between devices  3.72 us (5%)
    all_gather x1, blocking collectives, on_device(): every_row = lax.all_gather(own_right, 'gx', axis=0, tiled=True)  18 us
    all_gather x1, blocking collectives, on_device(): lax.all_gather(left_side, 'gy')  13.6 us
    reduce_scatter x1, waiting for transfers between devices, on_device(): lax.psum_scatter(jnp.einsum('jkc,ikc->jic', row_panel, left_slab, preferr...  7.61 us
    all_to_all x1, starting transfers between devices, on_device(): lax.all_to_all(every_row, 'gy', split_axis=0, concat_axis=1, tiled=True)  3.72 us
    all_to_all x2, local copies, waits for them, and re-layouts, on_device(): lax.all_to_all(every_row, 'gy', split_axis=0, concat_axis=1, tiled=True)  2.59 us
    reduce_sum x2, other arithmetic, normalize(): variance = jnp.mean(centered * centered, axis=-1, keepdims=True)  2.36 us
    transpose x1, local copies, waits for them, and re-layouts, on_device(): jnp.einsum('jkc,ikc->jic', row_panel, left_slab, preferred_element_type=j...  2.21 us
    reduce_sum x2, other arithmetic, normalize(): average = jnp.mean(values, axis=-1, keepdims=True)  2.16 us
  transfers between devices with their start and end apart: 2, of which 1 were waited for; matrix products, arithmetic and copies ran while one was open for 3% of the time, Pallas kernels for 0%

profile of v1, /device:TPU:0, one launch (start us, length us, event | category | flops | bytes accessed | tf_op | source)
XLA Modules:
  0.0 74.4 jit_solution(11856309138088779389)
XLA Ops:
  6.5 0.0 copy-start
  6.5 1.1 %convert_reduce_fusion = f32[32,16]{1,0:T(8,128)S(1)} fusion(bf16[32,16,128]{2,1,0:T(8,128)(2,1)} %param.9), kind=kLoop, calls=%fused_computation.8 | loop fusion | flops 130560 | bytes 133120 | tf_op jit(solution)/shard_map/reduce_sum | solution.py:8
  7.6 0.1 copy.56
  7.7 0.1 copy.57
  7.8 1.1 %fusion.6 = f32[32,16]{1,0:T(8,128)S(1)} fusion(bf16[32,16,128]{2,1,0:T(8,128)(2,1)} %param.9, f32[32,16]{1,0:T(8,128)S(1)} %copy.57), kind=kLoop, calls=%fused_computation.11 | loop fusion | flops 261632 | bytes 135168 | tf_op jit(solution)/shard_map/reduce_sum | solution.py:10
  8.9 0.1 copy.58
  9.0 0.1 copy.59
  9.1 0.7 convert_element_type.23
  9.8 0.1 copy.60
  9.9 0.0 copy-done
  9.9 1.3 %fusion.20 = f32[32,16,512]{2,1,0:T(8,128)S(1)} fusion(bf16[128,512]{1,0:T(8,128)(2,1)S(1)} %copy-done, bf16[32,16,128]{2,1,0:T(8,128)(2,1)} %param.9, f32[128]{0:T(128)} %param.12, f32[128]{0:T(128)} %param.11, f32[32,16]{1,0:T(8,128)S(1)} %copy.59, f32[32,16]{1,0:T(8,128)S(1)} %copy.57), kind=kOutput, calls=%fused_computation.33 | convolution fusion | flops 67502080 | bytes 1315840 | tf_op jit(solution)/shard_map/rwc,cd->rwd/dot_general | solution.py:17
  11.2 0.2 fusion.11
  11.3 18.0 %all_gather.11 = bf16[128,16,128]{2,1,0:T(8,128)(2,1)} all-gather(bf16[32,16,128]{2,1,0:T(8,128)(2,1)S(1)} %get-tuple-element.5), channel_id=1, replica_groups=mesh['gx'=4,'gy'=4,'gz'=2] {'gx'}, dimensions={0}, use_global_device_ids=true | all-gather | bytes 655360 | tf_op jit(solution)/shard_map/all_gather | solution.py:38
  29.3 3.7 %all-to-all-start = ((bf16[128,16,128]{2,1,0:T(8,128)(2,1)}), bf16[128,16,128]{2,1,0:T(8,128)(2,1)S(1)}, u32[]{:S(2)}, u32[]{:S(2)}) async-start(bf16[128,16,128]{2,1,0:T(8,128)(2,1)} %all_gather.11), calls=%async_computation | async-start | bytes 1048576 | tf_op jit(solution)/shard_map/all_to_all | solution.py:39
  33.1 0.0 reduce-scatter.2.cloned.1.call-start
  33.1 13.6 %all-gather = bf16[128,16,128]{2,1,0:T(8,128)(2,1)S(1)} all-gather(bf16[32,16,128]{2,1,0:T(8,128)(2,1)S(1)} %get-tuple-element.6), channel_id=2, replica_groups=mesh['gx'=4,'gy'=4,'gz'=2] {'gy'}, dimensions={0}, use_global_device_ids=true | all-gather | bytes 655360 | tf_op jit(solution)/shard_map/all_gather | solution.py:35
  46.7 0.1 copy.61
  46.8 1.6 %copy.63 = bf16[32,64,128]{1,0,2:T(8,128)(2,1)S(1)} copy(bf16[32,64,128]{2,1,0:T(8,128)(2,1)S(1)} %bitcast.28) | data formatting | bytes 1048576 | tf_op jit(solution)/shard_map/reshape | solution.py:35
  48.4 0.0 all-to-all-done
  48.4 0.1 copy.62
  48.5 2.5 %copy.64 = bf16[32,64,128]{1,0,2:T(8,128)(2,1)} copy(bf16[32,64,128]{2,1,0:T(8,128)(2,1)S(1)} %bitcast.29) | data formatting | bytes 1048576 | tf_op jit(solution)/shard_map/all_to_all | solution.py:39
  51.0 1.9 %convolution_bitcast_fusion = f32[32,32,128]{0,1,2:T(8,128)S(1)} fusion(bf16[32,64,128]{1,0,2:T(8,128)(2,1)S(1)} %copy.63, bf16[32,64,128]{1,0,2:T(8,128)(2,1)} %copy.64), kind=kOutput, calls=%fused_computation | convolution fusion | flops 16777216 | bytes 1572864 | tf_op jit(solution)/shard_map/jkc,ikc->jic/dot_general | solution.py:41
  52.9 0.0 copy-start.1
  52.9 0.0 copy-start.3
  52.9 0.0 copy-start.4
  52.9 0.0 copy-start.7
  52.9 0.0 copy-start.5
  53.0 0.0 copy-start.6
  53.0 2.2 %copy.65 = f32[32,32,128]{2,1,0:T(8,128)} copy(f32[32,32,128]{0,1,2:T(8,128)S(1)} %convolution_bitcast_fusion) | data formatting | bytes 1048576 | tf_op jit(solution)/shard_map/jkc,ikc->jic/transpose | solution.py:41
  55.2 0.0 copy-start.2
  55.2 0.0 reduce-scatter.2.cloned.1.call-update
  55.2 0.0 copy-done.1
  55.2 0.0 copy-done.3
  55.2 0.0 copy-done.4
  55.2 0.0 copy-done.7
  55.3 0.3 fusion.2
  55.6 7.6 %reduce-scatter.2.cloned.1.call-done = f32[16,32,128]{2,1,0:T(8,128)} async-done(((f32[32,32,128]{2,1,0:T(8,128)}), f32[16,32,128]{2,1,0:T(8,128)}) %reduce-scatter.2.cloned.1.call-update) | async-done | bytes 262160 | tf_op jit(solution)/shard_map/reduce_scatter | solution.py:40
  63.2 1.1 %bitcast_reduce_fusion = f32[32,16]{0,1:T(8,128)S(1)} fusion(f32[16,32,128]{2,1,0:T(8,128)} %reduce-scatter.2.cloned.1.call-done), kind=kLoop, calls=%fused_computation.30 | loop fusion | flops 65024 | bytes 264192 | tf_op jit(solution)/shard_map/reduce_sum | solution.py:8
  64.3 1.2 %multiply_reduce_fusion = f32[32,16]{0,1:T(8,128)S(1)} fusion(f32[16,32,128]{2,1,0:T(8,128)} %reduce-scatter.2.cloned.1.call-done, f32[32,16]{0,1:T(8,128)S(1)} %broadcast_multiply_fusion), kind=kLoop, calls=%fused_computation.32 | loop fusion | flops 196096 | bytes 266240 | tf_op jit(solution)/shard_map/reduce_sum | solution.py:10
  65.5 0.0 copy-done.5
  65.5 0.0 copy-done.6
  65.6 1.2 %add_convert_fusion = bf16[32,16,128]{2,0,1:T(8,128)(2,1)S(1)} fusion(f32[16,32,128]{2,1,0:T(8,128)} %reduce-scatter.2.cloned.1.call-done, f32[128]{0:T(128)S(1)} %copy-done.5, f32[128]{0:T(128)S(1)} %copy-done.6, f32[32,16]{0,1:T(8,128)S(1)} %add_rsqrt_fusion, f32[32,16]{0,1:T(8,128)S(1)} %broadcast_multiply_fusion), kind=kLoop, calls=%fused_computation.31 | loop fusion | flops 327680 | bytes 398336 | tf_op jit(solution)/shard_map/convert_element_type | solution.py:47
  66.7 0.0 copy-done.2
  66.7 0.8 %fusion.3 = bf16[32,16,128]{2,1,0:T(8,128)(2,1)} fusion(f32[32,16,128]{2,1,0:T(8,128)S(1)} %fusion.2, bf16[32,16,128]{2,0,1:T(8,128)(2,1)S(1)} %add_convert_fusion, bf16[128,128]{1,0:T(8,128)(2,1)S(1)} %copy-done.2), kind=kOutput, calls=%fused_computation.6 | convolution fusion | flops 16908288 | bytes 557056 | tf_op jit(solution)/shard_map/rwh,hc->rwc/dot_general | solution.py:51
  (4 shorter events, 0.0 us)
Async XLA Ops:
  6.5 3.3 %copy-start = (bf16[128,512]{1,0:T(8,128)(2,1)S(1)}, bf16[128,512]{1,0:T(8,128)(2,1)}, u32[]{:S(2)}) copy-start(bf16[128,512]{1,0:T(8,128)(2,1)} %param.13) | copy-start | bytes 393220
  29.3 19.1 %all-to-all-start = ((bf16[128,16,128]{2,1,0:T(8,128)(2,1)}), bf16[128,16,128]{2,1,0:T(8,128)(2,1)S(1)}, u32[]{:S(2)}, u32[]{:S(2)}) async-start(bf16[128,16,128]{2,1,0:T(8,128)(2,1)} %all_gather.11), calls=%async_computation | async-start | bytes 1048576 | tf_op jit(solution)/shard_map/all_to_all | solution.py:39
  33.1 30.1 %reduce-scatter.2.cloned.1.call-start = ((), (), s32[]{:S(2)}) async-start(), calls=%async_computation.2 | async-start | bytes 786432 | tf_op jit(solution)/shard_map/reduce_scatter | solution.py:40
  52.9 2.3 %copy-start.1 = (bf16[32,16,128]{2,1,0:T(8,128)(2,1)S(1)}, bf16[32,16,128]{2,1,0:T(8,128)(2,1)}, u32[]{:S(2)}) copy-start(bf16[32,16,128]{2,1,0:T(8,128)(2,1)} %param.9) | copy-start | bytes 393220
  52.9 2.3 %copy-start.3 = (f32[128]{0:T(128)S(1)}, f32[128]{0:T(128)}, u32[]{:S(2)}) copy-start(f32[128]{0:T(128)} %param.12) | copy-start | bytes 1540
  52.9 2.3 %copy-start.4 = (f32[128]{0:T(128)S(1)}, f32[128]{0:T(128)}, u32[]{:S(2)}) copy-start(f32[128]{0:T(128)} %param.11) | copy-start | bytes 1540
  52.9 2.3 %copy-start.7 = (bf16[128,128]{1,0:T(8,128)(2,1)S(1)}, bf16[128,128]{1,0:T(8,128)(2,1)}, u32[]{:S(2)}) copy-start(bf16[128,128]{1,0:T(8,128)(2,1)} %param.14) | copy-start | bytes 98308
  52.9 12.6 %copy-start.5 = (f32[128]{0:T(128)S(1)}, f32[128]{0:T(128)}, u32[]{:S(2)}) copy-start(f32[128]{0:T(128)} %param.16) | copy-start | bytes 1540
  53.0 12.6 %copy-start.6 = (f32[128]{0:T(128)S(1)}, f32[128]{0:T(128)}, u32[]{:S(2)}) copy-start(f32[128]{0:T(128)} %param.15) | copy-start | bytes 1540
  55.2 11.5 %copy-start.2 = (bf16[128,128]{1,0:T(8,128)(2,1)S(1)}, bf16[128,128]{1,0:T(8,128)(2,1)}, u32[]{:S(2)}) copy-start(bf16[128,128]{1,0:T(8,128)(2,1)} %param.17) | copy-start | bytes 98308
Sparse Core Ops, SparseCore 0:
  55.3 7.8 reduce-scatter.1
